TPU v7x, 256 devices: a whole 4x4x8 slice. The times are simulated.
256 devices in a mesh: section: 32 (over y, x, z_lo), tensor: 8 (over z_hi, core).
Axes of the slice: x: 4, y: 4, z: 8 (z_hi: 4, z_lo: 2; z = z_hi * 2 + z_lo), core: 2. Of those that a mesh axis runs over, the one named last changes fastest.
Arguments:
- hidden_in: bfloat16 [128, 8192], P(None, 'tensor'), may hold values from -36 to 36
- segment_ids: int32 [4, 32], replicated, may hold values from 0 to 7, never falling along the last dimension, each value on 1 to 8 neighbouring positions
- segment_job: int32 [4, 8], replicated, may hold values from 0 to 5
- job_adapter: int32 [6], replicated, may hold values from 0 to 3
- owner: int32 [32], P('section'), may hold values from 0 to 7
- frozen: bfloat16 [32, 8192, 4096], P('section', None, 'tensor'), may hold values from -0.0625 to 0.0625
- norm_gain: bfloat16 [32, 4096], P('section'), may hold values from 0.3984375 to 1.59375
- inbox_down: bfloat16 [32, 8, 4096, 128], P('section', 'tensor'), may hold values from -0.0625 to 0.0625
- inbox_up: bfloat16 [32, 8, 128, 4096], P('section', 'tensor'), may hold values from -1 to 1
Outputs:
- section_out: bfloat16 [32, 128, 4096], P('section', None, 'tensor')
Inputs may be any that keep to these rules, and one draw needn't show every extreme that they name: `segment_ids`: within each micro-batch the segment numbers never fall, and each of the 8 segments has 1 to 8 tokens.
All inputs are finite; a program needn't handle non-finite values.
Results may differ from a plain program's by a relative error of at most 0.02.
Values may be sent and summed in bfloat16 or wider, within the bound.
No kernel may reach another device: no remote copies, remote signals or barrier semaphores. Data moves between devices by JAX's collectives and lax.ppermute only.
A program may use at most 64 MiB of HBM per device.

v0:
```python
import functools

import jax
import jax.numpy as jnp
from jax import lax
from jax.experimental import pallas as pl
from jax.experimental.pallas import tpu as pltpu
from jax.sharding import PartitionSpec as P

R = 32
LANES = 128
SUB = 8
epsilon = 1e-05
row = 4
AXES = ("section", "tensor")


def routed(value, levels, chips, route):
    def place(level, chip, core):
        section = 2 * (level % levels) + chip % 2
        return section * chips + (chip % chips) // 2 * 2 + core

    pairs = []
    for level in range(levels):
        for chip in range(chips):
            for core in range(2):
                target = route(level, chip, core)
                if target is not None:
                    pairs.append((place(level, chip, core), place(*target)))
    return lax.ppermute(value, AXES, pairs)


def bring(columns, far_w, static, sent, parity):
    quads, cores, _, cols, _ = columns.shape

    def kernel(static, columns, far_w, sent, out_a, out_b, done):
        copies = [pltpu.make_async_copy(far_w, out_b, done.at[quads * cores])]
        for q in range(quads):
            for core in range(cores):
                source = columns.at[q, core, static[6]]
                target = out_a.at[q, pl.ds(core * cols, cols), :]
                copies.append(pltpu.make_async_copy(source, target, done.at[q * cores + core]))

        @pl.when(static[5] & 1 != parity)
        def _():
            for copy in copies:
                copy.start()
            for copy in copies:
                copy.wait()

    held = pltpu.VMEM(far_w.shape, far_w.dtype)
    return pl.pallas_call(
        kernel,
        out_shape=(held, held),
        in_specs=[pl.BlockSpec(memory_space=pltpu.SMEM)] + [pl.BlockSpec(memory_space=pl.ANY)] * 3,
        out_specs=(pl.BlockSpec(memory_space=pltpu.VMEM),) * 2,
        scratch_shapes=[pltpu.SemaphoreType.DMA((quads * cores + 1,))],
        compiler_params=pltpu.CompilerParams(vmem_limit_bytes=1 << 20),
        cost_estimate=pl.CostEstimate(flops=1 << 32, bytes_accessed=4 * far_w.size, transcendentals=0),
        name="bring",
    )(static, columns, far_w, sent)


def stage(columns, static, after):
    quads, cores, _, cols, _ = columns.shape

    def kernel(static, columns, after, out, held, came, went):
        inward, outward = [], []
        for q in range(quads):
            for core in range(cores):
                i = q * cores + core
                rows_at = pl.ds(core * cols, cols)
                source = columns.at[q, core, 1 - static[6]]
                inward.append(pltpu.make_async_copy(source, held.at[q, rows_at, :], came.at[i]))
                outward.append(pltpu.make_async_copy(held.at[q, rows_at, :], out.at[q, rows_at, :], went.at[i]))
        for copy in inward:
            copy.start()
        for copy, onward in zip(inward, outward):
            copy.wait()
            onward.start()
        for onward in outward:
            onward.wait()

    return pl.pallas_call(
        kernel,
        out_shape=jax.ShapeDtypeStruct((quads, cores * cols, cols), columns.dtype),
        in_specs=[pl.BlockSpec(memory_space=pltpu.SMEM)] + [pl.BlockSpec(memory_space=pl.ANY)] * 2,
        out_specs=pl.BlockSpec(memory_space=pl.ANY),
        scratch_shapes=[
            pltpu.VMEM((quads, cores * cols, cols), columns.dtype),
            pltpu.SemaphoreType.DMA((quads * cores,)),
            pltpu.SemaphoreType.DMA((quads * cores,)),
        ],
        compiler_params=pltpu.CompilerParams(vmem_limit_bytes=8 << 20),
        cost_estimate=pl.CostEstimate(flops=1 << 32, bytes_accessed=columns.size, transcendentals=0),
        name="stage",
    )(static, columns, after)


def dot(left, right):
    return jnp.dot(left, right, preferred_element_type=jnp.float32)


def partial_kernel(rows, order, more, parity, static, *refs):
    @pl.when(static[5] & 1 != parity)
    def _():
        partial_body(rows, order, more, static, *refs)


def partial_body(rows, order, more, static, *refs):
    blocks_in, (gain, own_w, other_w), out = refs[: len(order)], refs[len(order) : len(order) + 3], refs[-1]
    core = static[4]
    cols = own_w.shape[2]
    blocks = 2 * cols // LANES
    own_sum = other_sum = squares = low = None
    for k, block in zip(order, blocks_in):
        place = static[k]
        parts = []
        for j in range(blocks):
            x = block[j * rows : (j + 1) * rows, :].astype(jnp.float32)
            squares = x * x if squares is None else squares + x * x
            parts.append((x * gain[place, j : j + 1, :]).astype(jnp.bfloat16))
        scaled = jnp.concatenate(parts, axis=1)
        low_k = block[blocks * rows :, :].astype(jnp.float32)
        own_k = dot(scaled, own_w[place])
        other_k = dot(scaled, other_w[place])
        own_sum = own_k if own_sum is None else own_sum + own_k
        other_sum = other_k if other_sum is None else other_sum + other_k
        low = low_k if low is None else low + low_k
    own_at = pl.ds(pl.multiple_of(core * rows, SUB), rows)
    other_at = pl.ds(pl.multiple_of((1 - core) * rows, SUB), rows)
    total = jnp.broadcast_to(jnp.sum(squares, axis=1, keepdims=True), (rows, LANES))
    if more:
        before = refs[len(order) + 3]
        own_sum = own_sum + before[own_at, :]
        other_sum = other_sum + before[other_at, :]
        low = low + before[2 * rows : 2 * rows + SUB, 0:LANES]
    out[own_at, :] = own_sum
    out[other_at, :] = other_sum
    out[2 * rows : 2 * rows + SUB, 0:LANES] = low
    for g in range(rows // SUB):
        at = slice(2 * rows + SUB, 2 * rows + 2 * SUB), slice(g * LANES, (g + 1) * LANES)
        part = total[g * SUB : (g + 1) * SUB]
        out[at] = part + before[at] if more else part


def finish_kernel(rows, units, levels, width, parity, static, *refs):
    @pl.when(static[5] & 1 != parity)
    def _():
        finish_body(rows, units, levels, width, static, *refs)


def finish_body(
    rows, units, levels, width, static, turn, own_e, far_e, own_x, far_x, slot, up, down, source, results_in, sent, results
):
    core, level = static[4], static[5]
    step = turn[0]
    cols = own_e.shape[1]
    blocks = 2 * cols // LANES
    groups = rows // SUB
    behind = step - level
    active = jnp.logical_and(behind >= 0, jnp.logical_and(behind < 2 * units, behind % 2 == 0))
    feeding = jnp.logical_and(level == levels - 1, jnp.logical_and(step % 2 != 0, step + 1 < 2 * units))
    unit = jnp.where(feeding, (step + 1) // 2, jnp.clip(behind // 2, 0, units - 1))
    at = pl.multiple_of(unit * rows, SUB)
    token_slot = slot[pl.ds(at, rows), :]
    lane_slot = lax.broadcasted_iota(jnp.int32, (SUB, LANES), 1) // R
    low = own_e[2 * rows : 2 * rows + SUB, 0:LANES] + far_e[2 * rows : 2 * rows + SUB, 0:LANES]
    turned = [low] + [pltpu.roll(low, s * R, 1) for s in range(1, 4)]
    scales, kept = [], []
    for g in range(groups):
        here = pl.ds(g * LANES, LANES)
        squares = own_e[2 * rows + SUB : 2 * rows + 2 * SUB, here] + far_e[2 * rows + SUB : 2 * rows + 2 * SUB, here]
        scale = lax.rsqrt(squares / width + epsilon)
        spread = turned[(0 - g) % 4]
        for a in range(1, 4):
            spread = jnp.where(lane_slot == a, turned[(a - g) % 4], spread)
        mine = lane_slot == token_slot[g * SUB : (g + 1) * SUB]
        kept.append(jnp.where(mine, spread * scale, 0.0))
        scales.append(scale)
    scale = jnp.concatenate(scales, axis=0)
    kept = jnp.concatenate(kept, axis=0).astype(jnp.bfloat16)
    fresh = []
    first = core == 0
    for j in range(blocks):
        row = j * rows
        x = jnp.where(first, own_x[row : row + rows, :], far_x[row : row + rows, :]).astype(jnp.float32)
        half, lane = (0, j * LANES) if j * LANES < cols else (rows, j * LANES - cols)
        product = own_e[half : half + rows, lane : lane + LANES] + far_e[half : half + rows, lane : lane + LANES]
        added = dot(kept, up[j * LANES : (j + 1) * LANES, :])
        y = (x + scale * product + added).astype(jnp.bfloat16)
        fed = source[pl.ds(pl.multiple_of(unit * (blocks * rows) + row, SUB), rows), :]
        fresh.append(jnp.where(feeding, fed, y))
    for j in range(blocks):
        sent[j * rows : (j + 1) * rows, :] = fresh[j]
    next_low = dot(jnp.concatenate(fresh, axis=1), down[...])
    packed = None
    for g in range(groups):
        mine = lane_slot == token_slot[g * SUB : (g + 1) * SUB]
        picked = jnp.where(mine, next_low[g * SUB : (g + 1) * SUB], 0.0)
        picked = picked + pltpu.roll(picked, 2 * R, 1)
        picked = picked + pltpu.roll(picked, R, 1)
        packed = picked if packed is None else jnp.where(lane_slot == g, picked, packed)
    sent[blocks * rows :, :] = packed.astype(jnp.bfloat16)

    @pl.when(active)
    def _():
        for i in range(blocks // 2):
            mine = jnp.where(first, fresh[i], fresh[blocks // 2 + i])
            results[pl.ds(at, rows), i * LANES : (i + 1) * LANES] = mine


def relay(
    hidden_in, segment_ids, segment_job, job_adapter, owner, frozen, norm_gain, inbox_down, inbox_up
):
    chips = lax.axis_size("tensor")
    levels = lax.axis_size("section") // 2
    cols = frozen.shape[2]
    half_width = norm_gain.shape[1]
    units, rows = segment_ids.shape
    quads = chips // 2
    pair = 2 * cols
    blocks = pair // LANES
    position = lax.axis_index("section")
    side, level = position & 1, position >> 1
    shard = lax.axis_index("tensor")
    spot, core = shard >> 1, shard & 1
    first = core == 0
    move = functools.partial(routed, levels=levels, chips=chips)

    def swap(value):
        return move(value, route=lambda p, z, c: (p, z, 1 - c))

    arriving = side ^ core
    places = [(spot - k - core * (1 - side)) & (quads - 1) for k in range(quads)]
    static = jnp.stack(places + [core, level, arriving]).astype(jnp.int32)

    down = inbox_down[0, 0]
    up = inbox_up[0, 0].reshape(LANES, half_width // LANES, LANES).transpose(1, 0, 2).reshape(half_width, LANES)
    from_core = swap(jnp.where(first, down, up))
    chip_has = jnp.where(owner[0] & 1 == core, jnp.where(first, up, down), from_core)
    owner_next = move(owner, route=lambda p, z, c: (p - 1, z, c))
    gain_next = move(norm_gain, route=lambda p, z, c: (p - 1, z, c))
    gain_other = move(norm_gain, route=lambda p, z, c: (p, z ^ 1, c))
    wanted = jnp.where(first, owner[0], owner_next[0]) >> 1
    adapter_part = None
    chunks = [lax.dynamic_slice_in_dim(chip_has, ((spot + k) & (quads - 1)) * pair, pair, 0) for k in range(quads)]
    for k in (2, 1, 3, 0):
        came = move(chunks[k], route=lambda p, z, c, k=k: (p - c, z + 2 * k, c))
        hit = (spot - k) & (quads - 1) == wanted
        adapter_part = came if adapter_part is None else jnp.where(hit, came, adapter_part)
    adapter_other = swap(adapter_part)
    up_pair = jnp.where(first, adapter_part, adapter_other)
    down_pair = jnp.where(first, adapter_other, adapter_part)
    gain_rows = lax.dynamic_slice_in_dim(gain_next[0], spot * pair, pair, 0).astype(jnp.float32)
    down_pair = (down_pair.astype(jnp.float32) * gain_rows[:, None]).astype(jnp.bfloat16)
    gain = jnp.where(first, norm_gain, gain_other).reshape(quads, blocks, LANES).astype(jnp.float32)

    by_side = frozen[0].reshape(quads, 2, 2, cols, cols)
    far_w = stage(by_side, static, chunks[2])
    other_w = swap(far_w)

    own_half = lax.dynamic_slice_in_dim(hidden_in, side * cols, cols, 1)
    other_half = swap(own_half)
    both = jnp.concatenate([jnp.where(first, own_half, other_half), jnp.where(first, other_half, own_half)], axis=1)
    source = both.reshape(units, rows, blocks, LANES).transpose(0, 2, 1, 3).reshape(units * blocks * rows, LANES)

    seg_hit = segment_ids[:, :, None] == lax.broadcasted_iota(jnp.int32, (1, 1, segment_job.shape[1]), 2)
    token_job = jnp.sum(jnp.where(seg_hit, segment_job[:, None, :], 0), axis=2)
    job_hit = token_job[:, :, None] == lax.broadcasted_iota(jnp.int32, (1, 1, job_adapter.shape[0]), 2)
    token_slot = jnp.sum(jnp.where(job_hit, job_adapter[None, None, :], 0), axis=2)
    slot = jnp.broadcast_to(token_slot.reshape(units * rows, 1), (units * rows, LANES))
    slot = lax.optimization_barrier(slot)

    smem = pl.BlockSpec(memory_space=pltpu.SMEM)
    vmem = pl.BlockSpec(memory_space=pltpu.VMEM)
    payload = jax.ShapeDtypeStruct((blocks * rows + SUB, LANES), jnp.bfloat16)
    partial = jax.ShapeDtypeStruct((2 * rows + 2 * SUB, cols), jnp.float32)
    out_shape = jax.ShapeDtypeStruct((units * rows, cols), jnp.bfloat16)
    early, late = (0, 1), (2, 3)

    def multiply(order, more, parity):
        return pl.pallas_call(
            functools.partial(partial_kernel, rows, order, more, parity),
            out_shape=partial,
            in_specs=[smem] + [vmem] * (len(order) + 3 + more),
            out_specs=vmem,
            compiler_params=pltpu.CompilerParams(vmem_limit_bytes=16 << 20),
            cost_estimate=pl.CostEstimate(
                flops=len(order) * 2 * rows * pair * pair, bytes_accessed=len(order) * 2 * pair * pair, transcendentals=0
            ),
            name="multiply",
        )

    def finish(parity):
        return pl.pallas_call(
            functools.partial(finish_kernel, rows, units, levels, 2 * half_width, parity),
            out_shape=(payload, out_shape),
            in_specs=[smem, smem] + [vmem] * 9,
            out_specs=(vmem, vmem),
            input_output_aliases={10: 1},
            compiler_params=pltpu.CompilerParams(vmem_limit_bytes=16 << 20),
            name="finish",
        )

    def end(step, parity, own_e, far_e, own_x, far_x, results):
        turn = jnp.full((1,), step, jnp.int32)
        return finish(parity)(static, turn, own_e, far_e, own_x, far_x, slot, up_pair, down_pair, source, results)

    def half_step(step, parity, far_edges, sent, results):
        def sends(p):
            return p % 2 == parity and (p % row != row - 1 or p in far_edges)

        blocks_in = {
            k: move(sent, route=lambda p, z, c, k=k: (p + 1, z + 2 * k + c, c) if sends(p) else None)
            for k in early + late
        }
        far_x = swap(blocks_in[0])
        weights = gain, *bring(by_side, other_w, static, sent, parity)
        own_e = multiply(early, False, parity)(static, *[blocks_in[k] for k in early], *weights)
        own_e = multiply(late, True, parity)(static, *[blocks_in[k] for k in late], *weights, own_e)
        far_e = swap(own_e)
        return end(step, parity, own_e, far_e, blocks_in[0], far_x, results)

    nothing_e = jnp.zeros(partial.shape, partial.dtype)
    nothing_x = jnp.zeros(payload.shape, payload.dtype)
    carry = end(-1, 0, nothing_e, nothing_e, nothing_x, nothing_x, jnp.zeros(out_shape.shape, out_shape.dtype))

    def two_steps(far_edges, i, carry):
        carry = half_step(2 * i, 1, far_edges, *carry)
        return half_step(2 * i + 1, 0, far_edges, *carry)

    turns = (levels + 2 * units - 2) // 2
    begin = 0
    while begin < turns:
        end_of = turns if begin >= levels // 2 else begin + (2 if begin else 4)
        far_edges = set()
        for p in range(row - 1, levels, row):
            first_turn = 0 if p == levels - 1 else (p + 1) // 2
            if first_turn < end_of and begin < first_turn + units:
                far_edges.add(p)
        carry = lax.fori_loop(begin, end_of, functools.partial(two_steps, far_edges), carry)
        begin = end_of
    return carry[1][None]


def solution(mesh):
    return jax.shard_map(
        relay,
        mesh=mesh,
        in_specs=(
            P(None, "tensor"),
            P(),
            P(),
            P(),
            P("section"),
            P("section", None, "tensor"),
            P("section", None),
            P("section", "tensor", None, None),
            P("section", "tensor", None, None),
        ),
        out_specs=P("section", None, "tensor"),
        check_vma=False,
    )
```

profile of v0, /device:TPU:62, one launch (start us, length us, event | category | flops | bytes accessed | tf_op | source)
XLA Modules:
  0.0 443.0 jit_solution(13861048778453581090)
XLA Ops:
  14.0 5.3 %collective-permute-done.48 = s32[1]{0:T(128)} collective-permute-done((s32[1]{0:T(128)}, s32[1]{0:T(128)}, u32[]{:S(2)}, u32[]{:S(2)}) %collective-permute-start.48) | collective-permute-done | bytes 36 | tf_op jit(solution)/shard_map/ppermute | solution.py:30
  19.9 6.4 %collective-permute-start.53 = (bf16[1024,128]{1,0:T(8,128)(2,1)S(1)}, bf16[1024,128]{1,0:T(8,128)(2,1)S(1)}, u32[]{:S(2)}, u32[]{:S(2)}) collective-permute-start(bf16[1024,128]{1,0:T(8,128)(2,1)S(1)} %get-tuple-element.803.after), channel_id=1, source_target_pairs={{0,4},{1,245},{8,12},{9,253},{2,6},{3,247},{10,14},{11,255},{4,0},... | collective-permute-start | bytes 786440 | tf_op jit(solution)/shard_map/ppermute | solution.py:30
  30.0 7.0 %collective-permute-start.56 = (bf16[128,512]{1,0:T(8,128)(2,1)S(1)}, bf16[128,512]{1,0:T(8,128)(2,1)S(1)}, u32[]{:S(2)}, u32[]{:S(2)}) collective-permute-start(bf16[128,512]{1,0:T(8,128)(2,1)S(1)} %constant_dynamic-slice_fusion), channel_id=1, source_target_pairs={{0,1},{1,0},{8,9},{9,8},{2,3},{3,2},{10,11},{11,10},{4,5},{5,4},{1... | collective-permute-start | bytes 393224 | tf_op jit(solution)/shard_map/ppermute | solution.py:30
  36.9 4.7 %collective-permute-done.51 = bf16[1024,128]{1,0:T(8,128)(2,1)S(1)} collective-permute-done((bf16[1024,128]{1,0:T(8,128)(2,1)S(1)}, bf16[1024,128]{1,0:T(8,128)(2,1)S(1)}, u32[]{:S(2)}, u32[]{:S(2)}) %collective-permute-start.51) | collective-permute-done | bytes 262176 | tf_op jit(solution)/shard_map/ppermute | solution.py:30
  41.7 6.6 %collective-permute-done.52 = bf16[1024,128]{1,0:T(8,128)(2,1)S(1)} collective-permute-done((bf16[1024,128]{1,0:T(8,128)(2,1)S(1)}, bf16[1024,128]{1,0:T(8,128)(2,1)S(1)}, u32[]{:S(2)}, u32[]{:S(2)}) %collective-permute-start.52) | collective-permute-done | bytes 262176 | tf_op jit(solution)/shard_map/ppermute | solution.py:30
  53.3 146.4 %while.60 = (s32[]{:T(128)}, bf16[264,128]{1,0:T(8,128)(2,1)S(1)}, bf16[128,512]{1,0:T(8,128)(2,1)S(1)}, s32[7]{0:T(128)S(1)}, bf16[4,2,2,512,512]{4,3,2,1,0:T(8...) while((s32[]{:T(128)}, bf16[264,128]{1,0:T(8,128)(2,1)S(1)}, ...), condition=%wide.region_3.4_spmd, body=%wide.region_2.3_spmd.sunk | while | flops 9126805504 | bytes 37569140 | solution.py:342
  80.1 5.3 %collective-permute-done.9.refs_1_ = bf16[264,128]{1,0:T(8,128)(2,1)S(1)} collective-permute-done((bf16[264,128]{1,0:T(8,128)(2,1)S(1)}, bf16[264,128]{1,0:T(8,128)(2,1)S(1)}, u32[]{:S(2)}, u32[]{:S(2)}) %collective-permute-start.9) | collective-permute-done | bytes 67616 | tf_op jit(solution)/shard_map/while/body/eval_jaxpr/ppermute | solution.py:30
  199.7 65.6 %while.61 = (s32[]{:T(128)}, bf16[264,128]{1,0:T(8,128)(2,1)S(1)}, bf16[128,512]{1,0:T(8,128)(2,1)S(1)}, s32[7]{0:T(128)S(1)}, bf16[4,2,2,512,512]{4,3,2,1,0:T(8...) while((s32[]{:T(128)}, bf16[264,128]{1,0:T(8,128)(2,1)S(1)}, ...), condition=%wide.region_5.6_spmd, body=%wide.region_4.5_spmd.sunk | while | flops 9126805504 | bytes 37569160 | solution.py:342
  215.6 4.5 %collective-permute-done.20.refs_0_.refs_3_ = bf16[264,128]{1,0:T(8,128)(2,1)S(1)} collective-permute-done((bf16[264,128]{1,0:T(8,128)(2,1)S(1)}, bf16[264,128]{1,0:T(8,128)(2,1)S(1)}, u32[]{:S(2)}, u32[]{:S(2)}) %collective-permute-start.20) | collective-permute-done | bytes 67616 | tf_op jit(solution)/shard_map/while/body/eval_jaxpr/ppermute | solution.py:30
  220.2 6.5 %collective-permute-done.21.refs_1_ = bf16[264,128]{1,0:T(8,128)(2,1)S(1)} collective-permute-done((bf16[264,128]{1,0:T(8,128)(2,1)S(1)}, bf16[264,128]{1,0:T(8,128)(2,1)S(1)}, u32[]{:S(2)}, u32[]{:S(2)}) %collective-permute-start.21) | collective-permute-done | bytes 67616 | tf_op jit(solution)/shard_map/while/body/eval_jaxpr/ppermute | solution.py:30
  248.3 5.0 %collective-permute-done.20.refs_0_.refs_3_ = bf16[264,128]{1,0:T(8,128)(2,1)S(1)} collective-permute-done((bf16[264,128]{1,0:T(8,128)(2,1)S(1)}, bf16[264,128]{1,0:T(8,128)(2,1)S(1)}, u32[]{:S(2)}, u32[]{:S(2)}) %collective-permute-start.20) | collective-permute-done | bytes 67616 | tf_op jit(solution)/shard_map/while/body/eval_jaxpr/ppermute | solution.py:30
  253.2 6.7 %collective-permute-done.21.refs_1_ = bf16[264,128]{1,0:T(8,128)(2,1)S(1)} collective-permute-done((bf16[264,128]{1,0:T(8,128)(2,1)S(1)}, bf16[264,128]{1,0:T(8,128)(2,1)S(1)}, u32[]{:S(2)}, u32[]{:S(2)}) %collective-permute-start.21) | collective-permute-done | bytes 67616 | tf_op jit(solution)/shard_map/while/body/eval_jaxpr/ppermute | solution.py:30
  265.4 68.5 %while.62 = (s32[]{:T(128)}, bf16[264,128]{1,0:T(8,128)(2,1)S(1)}, bf16[128,512]{1,0:T(8,128)(2,1)S(1)}, s32[7]{0:T(128)S(1)}, bf16[4,2,2,512,512]{4,3,2,1,0:T(8...) while((s32[]{:T(128)}, bf16[264,128]{1,0:T(8,128)(2,1)S(1)}, ...), condition=%wide.region_7.8_spmd, body=%wide.region_6.7_spmd.sunk | while | flops 9126805504 | bytes 37569160 | solution.py:342
  281.4 4.7 %collective-permute-done.32.refs_0_.refs_3_ = bf16[264,128]{1,0:T(8,128)(2,1)S(1)} collective-permute-done((bf16[264,128]{1,0:T(8,128)(2,1)S(1)}, bf16[264,128]{1,0:T(8,128)(2,1)S(1)}, u32[]{:S(2)}, u32[]{:S(2)}) %collective-permute-start.32) | collective-permute-done | bytes 67616 | tf_op jit(solution)/shard_map/while/body/eval_jaxpr/ppermute | solution.py:30
  286.1 6.2 %collective-permute-done.33.refs_1_ = bf16[264,128]{1,0:T(8,128)(2,1)S(1)} collective-permute-done((bf16[264,128]{1,0:T(8,128)(2,1)S(1)}, bf16[264,128]{1,0:T(8,128)(2,1)S(1)}, u32[]{:S(2)}, u32[]{:S(2)}) %collective-permute-start.33) | collective-permute-done | bytes 67616 | tf_op jit(solution)/shard_map/while/body/eval_jaxpr/ppermute | solution.py:30
  313.8 7.6 %collective-permute-done.32.refs_0_.refs_3_ = bf16[264,128]{1,0:T(8,128)(2,1)S(1)} collective-permute-done((bf16[264,128]{1,0:T(8,128)(2,1)S(1)}, bf16[264,128]{1,0:T(8,128)(2,1)S(1)}, u32[]{:S(2)}, u32[]{:S(2)}) %collective-permute-start.32) | collective-permute-done | bytes 67616 | tf_op jit(solution)/shard_map/while/body/eval_jaxpr/ppermute | solution.py:30
  321.5 6.4 %collective-permute-done.33.refs_1_ = bf16[264,128]{1,0:T(8,128)(2,1)S(1)} collective-permute-done((bf16[264,128]{1,0:T(8,128)(2,1)S(1)}, bf16[264,128]{1,0:T(8,128)(2,1)S(1)}, u32[]{:S(2)}, u32[]{:S(2)}) %collective-permute-start.33) | collective-permute-done | bytes 67616 | tf_op jit(solution)/shard_map/while/body/eval_jaxpr/ppermute | solution.py:30
  333.9 108.4 %while.63 = (s32[]{:T(128)}, bf16[264,128]{1,0:T(8,128)(2,1)S(1)}, bf16[128,512]{1,0:T(8,128)(2,1)S(1)}, s32[7]{0:T(128)S(1)}, bf16[4,2,2,512,512]{4,3,2,1,0:T(8...) while((s32[]{:T(128)}, bf16[264,128]{1,0:T(8,128)(2,1)S(1)}, ...), condition=%wide.region_9.10_spmd, body=%wide.region_8.9_spmd.sunk | while | flops 9126805504 | bytes 37569160 | solution.py:342
  349.8 7.3 %collective-permute-done.44.refs_0_.refs_3_ = bf16[264,128]{1,0:T(8,128)(2,1)S(1)} collective-permute-done((bf16[264,128]{1,0:T(8,128)(2,1)S(1)}, bf16[264,128]{1,0:T(8,128)(2,1)S(1)}, u32[]{:S(2)}, u32[]{:S(2)}) %collective-permute-start.44) | collective-permute-done | bytes 67616 | tf_op jit(solution)/shard_map/while/body/eval_jaxpr/ppermute | solution.py:30
  357.0 6.3 %collective-permute-done.45.refs_1_ = bf16[264,128]{1,0:T(8,128)(2,1)S(1)} collective-permute-done((bf16[264,128]{1,0:T(8,128)(2,1)S(1)}, bf16[264,128]{1,0:T(8,128)(2,1)S(1)}, u32[]{:S(2)}, u32[]{:S(2)}) %collective-permute-start.45) | collective-permute-done | bytes 67616 | tf_op jit(solution)/shard_map/while/body/eval_jaxpr/ppermute | solution.py:30
  385.3 8.2 %collective-permute-done.44.refs_0_.refs_3_ = bf16[264,128]{1,0:T(8,128)(2,1)S(1)} collective-permute-done((bf16[264,128]{1,0:T(8,128)(2,1)S(1)}, bf16[264,128]{1,0:T(8,128)(2,1)S(1)}, u32[]{:S(2)}, u32[]{:S(2)}) %collective-permute-start.44) | collective-permute-done | bytes 67616 | tf_op jit(solution)/shard_map/while/body/eval_jaxpr/ppermute | solution.py:30
  393.5 7.0 %collective-permute-done.45.refs_1_ = bf16[264,128]{1,0:T(8,128)(2,1)S(1)} collective-permute-done((bf16[264,128]{1,0:T(8,128)(2,1)S(1)}, bf16[264,128]{1,0:T(8,128)(2,1)S(1)}, u32[]{:S(2)}, u32[]{:S(2)}) %collective-permute-start.45) | collective-permute-done | bytes 67616 | tf_op jit(solution)/shard_map/while/body/eval_jaxpr/ppermute | solution.py:30
  421.8 8.1 %collective-permute-done.44.refs_0_.refs_3_ = bf16[264,128]{1,0:T(8,128)(2,1)S(1)} collective-permute-done((bf16[264,128]{1,0:T(8,128)(2,1)S(1)}, bf16[264,128]{1,0:T(8,128)(2,1)S(1)}, u32[]{:S(2)}, u32[]{:S(2)}) %collective-permute-start.44) | collective-permute-done | bytes 67616 | tf_op jit(solution)/shard_map/while/body/eval_jaxpr/ppermute | solution.py:30
  429.9 6.4 %collective-permute-done.45.refs_1_ = bf16[264,128]{1,0:T(8,128)(2,1)S(1)} collective-permute-done((bf16[264,128]{1,0:T(8,128)(2,1)S(1)}, bf16[264,128]{1,0:T(8,128)(2,1)S(1)}, u32[]{:S(2)}, u32[]{:S(2)}) %collective-permute-start.45) | collective-permute-done | bytes 67616 | tf_op jit(solution)/shard_map/while/body/eval_jaxpr/ppermute | solution.py:30
  (393 shorter events, 313.2 us)
Async XLA Ops:
  12.0 41.3 %collective-permute-start.57 = (bf16[4,1024,512]{2,1,0:T(8,128)(2,1)}, bf16[4,1024,512]{2,1,0:T(8,128)(2,1)}, u32[]{:S(2)}, u32[]{:S(2)}) collective-permute-start(bf16[4,1024,512]{2,1,0:T(8,128)(2,1)} %stage.1), channel_id=1, source_target_pairs={{0,1},{1,0},{8,9},{9,8},{2,3},{3,2},{10,11},{11,10},{4,5},{5,4},{1... | collective-permute-start | bytes 12582920 | tf_op jit(solution)/shard_map/ppermute | solution.py:30
  19.9 28.4 %collective-permute-start.53 = (bf16[1024,128]{1,0:T(8,128)(2,1)S(1)}, bf16[1024,128]{1,0:T(8,128)(2,1)S(1)}, u32[]{:S(2)}, u32[]{:S(2)}) collective-permute-start(bf16[1024,128]{1,0:T(8,128)(2,1)S(1)} %get-tuple-element.803.after), channel_id=1, source_target_pairs={{0,4},{1,245},{8,12},{9,253},{2,6},{3,247},{10,14},{11,255},{4,0},... | collective-permute-start | bytes 786440 | tf_op jit(solution)/shard_map/ppermute | solution.py:30
  27.5 20.7 %collective-permute-start.52 = (bf16[1024,128]{1,0:T(8,128)(2,1)S(1)}, bf16[1024,128]{1,0:T(8,128)(2,1)S(1)}, u32[]{:S(2)}, u32[]{:S(2)}) collective-permute-start(bf16[1024,128]{1,0:T(8,128)(2,1)S(1)} %get-tuple-element.804), channel_id=1, source_target_pairs={{0,2},{1,243},{8,10},{9,251},{2,4},{3,245},{10,12},{11,253},{4,6},... | collective-permute-start | bytes 786440 | tf_op jit(solution)/shard_map/ppermute | solution.py:30
  30.0 20.7 %collective-permute-start.56 = (bf16[128,512]{1,0:T(8,128)(2,1)S(1)}, bf16[128,512]{1,0:T(8,128)(2,1)S(1)}, u32[]{:S(2)}, u32[]{:S(2)}) collective-permute-start(bf16[128,512]{1,0:T(8,128)(2,1)S(1)} %constant_dynamic-slice_fusion), channel_id=1, source_target_pairs={{0,1},{1,0},{8,9},{9,8},{2,3},{3,2},{10,11},{11,10},{4,5},{5,4},{1... | collective-permute-start | bytes 393224 | tf_op jit(solution)/shard_map/ppermute | solution.py:30
  207.7 18.9 %collective-permute-start.21 = (bf16[264,128]{1,0:T(8,128)(2,1)S(1)}, bf16[264,128]{1,0:T(8,128)(2,1)S(1)}, u32[]{:S(2)}, u32[]{:S(2)}) collective-permute-start(bf16[264,128]{1,0:T(8,128)(2,1)S(1)} %get-tuple-element.1097.sent), channel_id=1, source_target_pairs={{0,18},{1,27},{8,26},{9,21},{2,20},{3,29},{10,28},{11,23},{4,22},{... | collective-permute-start | bytes 202760 | tf_op jit(solution)/shard_map/while/body/eval_jaxpr/ppermute | solution.py:30
  209.0 19.0 %collective-permute-start.18 = (bf16[264,128]{1,0:T(8,128)(2,1)S(1)}, bf16[264,128]{1,0:T(8,128)(2,1)S(1)}, u32[]{:S(2)}, u32[]{:S(2)}) collective-permute-start(bf16[264,128]{1,0:T(8,128)(2,1)S(1)} %get-tuple-element.1097.sent), channel_id=1, source_target_pairs={{0,20},{1,29},{8,28},{9,23},{2,22},{3,31},{10,30},{11,17},{4,16},{... | collective-permute-start | bytes 202760 | tf_op jit(solution)/shard_map/while/body/eval_jaxpr/ppermute | solution.py:30
  210.3 18.0 %collective-permute-start.19 = (bf16[264,128]{1,0:T(8,128)(2,1)S(1)}, bf16[264,128]{1,0:T(8,128)(2,1)S(1)}, u32[]{:S(2)}, u32[]{:S(2)}) collective-permute-start(bf16[264,128]{1,0:T(8,128)(2,1)S(1)} %get-tuple-element.1097.sent), channel_id=1, source_target_pairs={{0,22},{1,31},{8,30},{9,17},{2,16},{3,25},{10,24},{11,19},{4,18},{... | collective-permute-start | bytes 202760 | tf_op jit(solution)/shard_map/while/body/eval_jaxpr/ppermute | solution.py:30
  240.4 19.6 %collective-permute-start.21 = (bf16[264,128]{1,0:T(8,128)(2,1)S(1)}, bf16[264,128]{1,0:T(8,128)(2,1)S(1)}, u32[]{:S(2)}, u32[]{:S(2)}) collective-permute-start(bf16[264,128]{1,0:T(8,128)(2,1)S(1)} %get-tuple-element.1097.sent), channel_id=1, source_target_pairs={{0,18},{1,27},{8,26},{9,21},{2,20},{3,29},{10,28},{11,23},{4,22},{... | collective-permute-start | bytes 202760 | tf_op jit(solution)/shard_map/while/body/eval_jaxpr/ppermute | solution.py:30
  241.7 19.7 %collective-permute-start.18 = (bf16[264,128]{1,0:T(8,128)(2,1)S(1)}, bf16[264,128]{1,0:T(8,128)(2,1)S(1)}, u32[]{:S(2)}, u32[]{:S(2)}) collective-permute-start(bf16[264,128]{1,0:T(8,128)(2,1)S(1)} %get-tuple-element.1097.sent), channel_id=1, source_target_pairs={{0,20},{1,29},{8,28},{9,23},{2,22},{3,31},{10,30},{11,17},{4,16},{... | collective-permute-start | bytes 202760 | tf_op jit(solution)/shard_map/while/body/eval_jaxpr/ppermute | solution.py:30
  243.0 18.4 %collective-permute-start.19 = (bf16[264,128]{1,0:T(8,128)(2,1)S(1)}, bf16[264,128]{1,0:T(8,128)(2,1)S(1)}, u32[]{:S(2)}, u32[]{:S(2)}) collective-permute-start(bf16[264,128]{1,0:T(8,128)(2,1)S(1)} %get-tuple-element.1097.sent), channel_id=1, source_target_pairs={{0,22},{1,31},{8,30},{9,17},{2,16},{3,25},{10,24},{11,19},{4,18},{... | collective-permute-start | bytes 202760 | tf_op jit(solution)/shard_map/while/body/eval_jaxpr/ppermute | solution.py:30
  273.5 18.8 %collective-permute-start.33 = (bf16[264,128]{1,0:T(8,128)(2,1)S(1)}, bf16[264,128]{1,0:T(8,128)(2,1)S(1)}, u32[]{:S(2)}, u32[]{:S(2)}) collective-permute-start(bf16[264,128]{1,0:T(8,128)(2,1)S(1)} %get-tuple-element.1116.sent), channel_id=1, source_target_pairs={{0,18},{1,27},{8,26},{9,21},{2,20},{3,29},{10,28},{11,23},{4,22},{... | collective-permute-start | bytes 202760 | tf_op jit(solution)/shard_map/while/body/eval_jaxpr/ppermute | solution.py:30
  274.8 18.9 %collective-permute-start.30 = (bf16[264,128]{1,0:T(8,128)(2,1)S(1)}, bf16[264,128]{1,0:T(8,128)(2,1)S(1)}, u32[]{:S(2)}, u32[]{:S(2)}) collective-permute-start(bf16[264,128]{1,0:T(8,128)(2,1)S(1)} %get-tuple-element.1116.sent), channel_id=1, source_target_pairs={{0,20},{1,29},{8,28},{9,23},{2,22},{3,31},{10,30},{11,17},{4,16},{... | collective-permute-start | bytes 202760 | tf_op jit(solution)/shard_map/while/body/eval_jaxpr/ppermute | solution.py:30
  305.9 22.0 %collective-permute-start.33 = (bf16[264,128]{1,0:T(8,128)(2,1)S(1)}, bf16[264,128]{1,0:T(8,128)(2,1)S(1)}, u32[]{:S(2)}, u32[]{:S(2)}) collective-permute-start(bf16[264,128]{1,0:T(8,128)(2,1)S(1)} %get-tuple-element.1116.sent), channel_id=1, source_target_pairs={{0,18},{1,27},{8,26},{9,21},{2,20},{3,29},{10,28},{11,23},{4,22},{... | collective-permute-start | bytes 202760 | tf_op jit(solution)/shard_map/while/body/eval_jaxpr/ppermute | solution.py:30
  307.2 22.2 %collective-permute-start.30 = (bf16[264,128]{1,0:T(8,128)(2,1)S(1)}, bf16[264,128]{1,0:T(8,128)(2,1)S(1)}, u32[]{:S(2)}, u32[]{:S(2)}) collective-permute-start(bf16[264,128]{1,0:T(8,128)(2,1)S(1)} %get-tuple-element.1116.sent), channel_id=1, source_target_pairs={{0,20},{1,29},{8,28},{9,23},{2,22},{3,31},{10,30},{11,17},{4,16},{... | collective-permute-start | bytes 202760 | tf_op jit(solution)/shard_map/while/body/eval_jaxpr/ppermute | solution.py:30
  308.5 21.3 %collective-permute-start.31 = (bf16[264,128]{1,0:T(8,128)(2,1)S(1)}, bf16[264,128]{1,0:T(8,128)(2,1)S(1)}, u32[]{:S(2)}, u32[]{:S(2)}) collective-permute-start(bf16[264,128]{1,0:T(8,128)(2,1)S(1)} %get-tuple-element.1116.sent), channel_id=1, source_target_pairs={{0,22},{1,31},{8,30},{9,17},{2,16},{3,25},{10,24},{11,19},{4,18},{... | collective-permute-start | bytes 202760 | tf_op jit(solution)/shard_map/while/body/eval_jaxpr/ppermute | solution.py:30
  341.9 21.5 %collective-permute-start.45 = (bf16[264,128]{1,0:T(8,128)(2,1)S(1)}, bf16[264,128]{1,0:T(8,128)(2,1)S(1)}, u32[]{:S(2)}, u32[]{:S(2)}) collective-permute-start(bf16[264,128]{1,0:T(8,128)(2,1)S(1)} %get-tuple-element.1135.sent), channel_id=1, source_target_pairs={{0,18},{1,27},{8,26},{9,21},{2,20},{3,29},{10,28},{11,23},{4,22},{... | collective-permute-start | bytes 202760 | tf_op jit(solution)/shard_map/while/body/eval_jaxpr/ppermute | solution.py:30
  343.2 21.5 %collective-permute-start.42 = (bf16[264,128]{1,0:T(8,128)(2,1)S(1)}, bf16[264,128]{1,0:T(8,128)(2,1)S(1)}, u32[]{:S(2)}, u32[]{:S(2)}) collective-permute-start(bf16[264,128]{1,0:T(8,128)(2,1)S(1)} %get-tuple-element.1135.sent), channel_id=1, source_target_pairs={{0,20},{1,29},{8,28},{9,23},{2,22},{3,31},{10,30},{11,17},{4,16},{... | collective-permute-start | bytes 202760 | tf_op jit(solution)/shard_map/while/body/eval_jaxpr/ppermute | solution.py:30
  344.5 20.9 %collective-permute-start.43 = (bf16[264,128]{1,0:T(8,128)(2,1)S(1)}, bf16[264,128]{1,0:T(8,128)(2,1)S(1)}, u32[]{:S(2)}, u32[]{:S(2)}) collective-permute-start(bf16[264,128]{1,0:T(8,128)(2,1)S(1)} %get-tuple-element.1135.sent), channel_id=1, source_target_pairs={{0,22},{1,31},{8,30},{9,17},{2,16},{3,25},{10,24},{11,19},{4,18},{... | collective-permute-start | bytes 202760 | tf_op jit(solution)/shard_map/while/body/eval_jaxpr/ppermute | solution.py:30
  377.4 23.1 %collective-permute-start.45 = (bf16[264,128]{1,0:T(8,128)(2,1)S(1)}, bf16[264,128]{1,0:T(8,128)(2,1)S(1)}, u32[]{:S(2)}, u32[]{:S(2)}) collective-permute-start(bf16[264,128]{1,0:T(8,128)(2,1)S(1)} %get-tuple-element.1135.sent), channel_id=1, source_target_pairs={{0,18},{1,27},{8,26},{9,21},{2,20},{3,29},{10,28},{11,23},{4,22},{... | collective-permute-start | bytes 202760 | tf_op jit(solution)/shard_map/while/body/eval_jaxpr/ppermute | solution.py:30
  378.7 23.2 %collective-permute-start.42 = (bf16[264,128]{1,0:T(8,128)(2,1)S(1)}, bf16[264,128]{1,0:T(8,128)(2,1)S(1)}, u32[]{:S(2)}, u32[]{:S(2)}) collective-permute-start(bf16[264,128]{1,0:T(8,128)(2,1)S(1)} %get-tuple-element.1135.sent), channel_id=1, source_target_pairs={{0,20},{1,29},{8,28},{9,23},{2,22},{3,31},{10,30},{11,17},{4,16},{... | collective-permute-start | bytes 202760 | tf_op jit(solution)/shard_map/while/body/eval_jaxpr/ppermute | solution.py:30
  380.0 21.9 %collective-permute-start.43 = (bf16[264,128]{1,0:T(8,128)(2,1)S(1)}, bf16[264,128]{1,0:T(8,128)(2,1)S(1)}, u32[]{:S(2)}, u32[]{:S(2)}) collective-permute-start(bf16[264,128]{1,0:T(8,128)(2,1)S(1)} %get-tuple-element.1135.sent), channel_id=1, source_target_pairs={{0,22},{1,31},{8,30},{9,17},{2,16},{3,25},{10,24},{11,19},{4,18},{... | collective-permute-start | bytes 202760 | tf_op jit(solution)/shard_map/while/body/eval_jaxpr/ppermute | solution.py:30
  413.9 22.5 %collective-permute-start.45 = (bf16[264,128]{1,0:T(8,128)(2,1)S(1)}, bf16[264,128]{1,0:T(8,128)(2,1)S(1)}, u32[]{:S(2)}, u32[]{:S(2)}) collective-permute-start(bf16[264,128]{1,0:T(8,128)(2,1)S(1)} %get-tuple-element.1135.sent), channel_id=1, source_target_pairs={{0,18},{1,27},{8,26},{9,21},{2,20},{3,29},{10,28},{11,23},{4,22},{... | collective-permute-start | bytes 202760 | tf_op jit(solution)/shard_map/while/body/eval_jaxpr/ppermute | solution.py:30
  415.2 22.5 %collective-permute-start.42 = (bf16[264,128]{1,0:T(8,128)(2,1)S(1)}, bf16[264,128]{1,0:T(8,128)(2,1)S(1)}, u32[]{:S(2)}, u32[]{:S(2)}) collective-permute-start(bf16[264,128]{1,0:T(8,128)(2,1)S(1)} %get-tuple-element.1135.sent), channel_id=1, source_target_pairs={{0,20},{1,29},{8,28},{9,23},{2,22},{3,31},{10,30},{11,17},{4,16},{... | collective-permute-start | bytes 202760 | tf_op jit(solution)/shard_map/while/body/eval_jaxpr/ppermute | solution.py:30
  416.5 21.8 %collective-permute-start.43 = (bf16[264,128]{1,0:T(8,128)(2,1)S(1)}, bf16[264,128]{1,0:T(8,128)(2,1)S(1)}, u32[]{:S(2)}, u32[]{:S(2)}) collective-permute-start(bf16[264,128]{1,0:T(8,128)(2,1)S(1)} %get-tuple-element.1135.sent), channel_id=1, source_target_pairs={{0,22},{1,31},{8,30},{9,17},{2,16},{3,25},{10,24},{11,19},{4,18},{... | collective-permute-start | bytes 202760 | tf_op jit(solution)/shard_map/while/body/eval_jaxpr/ppermute | solution.py:30
  (126 other events, 666.0 us)
where the time goes:
time: 448 us; the launch traced here: 443 us
  waiting for transfers between devices  170 us (38%)
  starting transfers between devices  147 us (33%)
  Pallas kernels  116 us (26%)
    ppermute x143, waiting for transfers between devices, routed(): return lax.ppermute(value, AXES, pairs)  170 us
    ppermute x143, starting transfers between devices, routed(): return lax.ppermute(value, AXES, pairs)  147 us
    pallas_call x22, Pallas kernels, bring(): pl.pallas_call(kernel, out_shape=(held, held), in_specs=[pl.BlockSpec(mem...  51 us
    pallas_call x22, Pallas kernels, half_step(): multiply(late, True, parity)  21.1 us
    pallas_call x22, Pallas kernels, half_step(): multiply(early, False, parity)  21 us
    pallas_call x23, Pallas kernels, end(): finish(parity)  18.8 us
  transfers between devices with their start and end apart: 143, of which 64 were waited for; matrix products, arithmetic and copies ran while one was open for 0% of the time, Pallas kernels for 17%

commit v1 on v0

--- a/solution.py
+++ b/solution.py
@@ -277,7 +277,7 @@
     payload = jax.ShapeDtypeStruct((blocks * rows + SUB, LANES), jnp.bfloat16)
     partial = jax.ShapeDtypeStruct((2 * rows + 2 * SUB, cols), jnp.float32)
     out_shape = jax.ShapeDtypeStruct((units * rows, cols), jnp.bfloat16)
-    early, late = (0, 1), (2, 3)
+    arrivals = (0, 1), (2,), (3,)
 
     def multiply(order, more, parity):
         return pl.pallas_call(
@@ -313,12 +313,15 @@
 
         blocks_in = {
             k: move(sent, route=lambda p, z, c, k=k: (p + 1, z + 2 * k + c, c) if sends(p) else None)
-            for k in early + late
+            for k in range(quads)
         }
         far_x = swap(blocks_in[0])
         weights = gain, *bring(by_side, other_w, static, sent, parity)
-        own_e = multiply(early, False, parity)(static, *[blocks_in[k] for k in early], *weights)
-        own_e = multiply(late, True, parity)(static, *[blocks_in[k] for k in late], *weights, own_e)
+        so_far = ()
+        for ks in arrivals:
+            blocks_now = [blocks_in[k] for k in ks]
+            so_far = (multiply(ks, len(so_far), parity)(static, *blocks_now, *weights, *so_far),)
+        (own_e,) = so_far
         far_e = swap(own_e)
         return end(step, parity, own_e, far_e, blocks_in[0], far_x, results)
 

time: 448 us -> 450 us (level)
  Pallas kernels: 116 us -> 129 us
  waiting for transfers between devices: 170 us -> 160 us
    pallas_call x44 -> x66, Pallas kernels: 42.1 us -> 55.4 us  [half_step(): multiply(ks, len(so_far), parity)(static, *blocks_now, *weights, *so_far)]
    ppermute x143, waiting for transfers between devices: 170 us -> 160 us  [routed(): return lax.ppermute(value, AXES, pairs)]
  transfers between devices with their start and end apart: 143 -> 143, of which waited for: 64 -> 64; matrix products, arithmetic and copies ran while one was open for 0% -> 0% of each run, Pallas kernels for 17% -> 20%
where the time goes in v1:
time: 450 us; the launch traced here: 446 us
  waiting for transfers between devices  160 us (36%)
  starting transfers between devices  147 us (33%)
  Pallas kernels  129 us (29%)
    ppermute x143, waiting for transfers between devices, routed(): return lax.ppermute(value, AXES, pairs)  160 us
    ppermute x143, starting transfers between devices, routed(): return lax.ppermute(value, AXES, pairs)  147 us
    pallas_call x66, Pallas kernels, half_step(): multiply(ks, len(so_far), parity)(static, *blocks_now, *weights, *so_far)  55.4 us
    pallas_call x22, Pallas kernels, bring(): pl.pallas_call(kernel, out_shape=(held, held), in_specs=[pl.BlockSpec(mem...  51 us
    pallas_call x23, Pallas kernels, end(): finish(parity)  18.8 us
  transfers between devices with their start and end apart: 143, of which 64 were waited for; matrix products, arithmetic and copies ran while one was open for 0% of the time, Pallas kernels for 20%

profile of v1, /device:TPU:62, one launch (start us, length us, event | category | flops | bytes accessed | tf_op | source)
XLA Modules:
  0.0 445.9 jit_solution(8208998050386579317)
XLA Ops:
  14.0 5.3 %collective-permute-done.48 = s32[1]{0:T(128)} collective-permute-done((s32[1]{0:T(128)}, s32[1]{0:T(128)}, u32[]{:S(2)}, u32[]{:S(2)}) %collective-permute-start.48) | collective-permute-done | bytes 36 | tf_op jit(solution)/shard_map/ppermute | solution.py:30
  19.9 6.4 %collective-permute-start.53 = (bf16[1024,128]{1,0:T(8,128)(2,1)S(1)}, bf16[1024,128]{1,0:T(8,128)(2,1)S(1)}, u32[]{:S(2)}, u32[]{:S(2)}) collective-permute-start(bf16[1024,128]{1,0:T(8,128)(2,1)S(1)} %get-tuple-element.803.after), channel_id=1, source_target_pairs={{0,4},{1,245},{8,12},{9,253},{2,6},{3,247},{10,14},{11,255},{4,0},... | collective-permute-start | bytes 786440 | tf_op jit(solution)/shard_map/ppermute | solution.py:30
  30.0 7.0 %collective-permute-start.56 = (bf16[128,512]{1,0:T(8,128)(2,1)S(1)}, bf16[128,512]{1,0:T(8,128)(2,1)S(1)}, u32[]{:S(2)}, u32[]{:S(2)}) collective-permute-start(bf16[128,512]{1,0:T(8,128)(2,1)S(1)} %constant_dynamic-slice_fusion), channel_id=1, source_target_pairs={{0,1},{1,0},{8,9},{9,8},{2,3},{3,2},{10,11},{11,10},{4,5},{5,4},{1... | collective-permute-start | bytes 393224 | tf_op jit(solution)/shard_map/ppermute | solution.py:30
  36.9 4.7 %collective-permute-done.51 = bf16[1024,128]{1,0:T(8,128)(2,1)S(1)} collective-permute-done((bf16[1024,128]{1,0:T(8,128)(2,1)S(1)}, bf16[1024,128]{1,0:T(8,128)(2,1)S(1)}, u32[]{:S(2)}, u32[]{:S(2)}) %collective-permute-start.51) | collective-permute-done | bytes 262176 | tf_op jit(solution)/shard_map/ppermute | solution.py:30
  41.7 6.6 %collective-permute-done.52 = bf16[1024,128]{1,0:T(8,128)(2,1)S(1)} collective-permute-done((bf16[1024,128]{1,0:T(8,128)(2,1)S(1)}, bf16[1024,128]{1,0:T(8,128)(2,1)S(1)}, u32[]{:S(2)}, u32[]{:S(2)}) %collective-permute-start.52) | collective-permute-done | bytes 262176 | tf_op jit(solution)/shard_map/ppermute | solution.py:30
  53.3 144.5 %while.60 = (s32[]{:T(128)}, bf16[264,128]{1,0:T(8,128)(2,1)S(1)}, bf16[128,512]{1,0:T(8,128)(2,1)S(1)}, s32[7]{0:T(128)S(1)}, bf16[4,2,2,512,512]{4,3,2,1,0:T(8...) while((s32[]{:T(128)}, bf16[264,128]{1,0:T(8,128)(2,1)S(1)}, ...), condition=%wide.region_3.4_spmd, body=%wide.region_2.3_spmd.sunk | while | flops 9126805504 | bytes 37569140 | solution.py:345
  80.1 5.2 %collective-permute-done.9.refs_1_ = bf16[264,128]{1,0:T(8,128)(2,1)S(1)} collective-permute-done((bf16[264,128]{1,0:T(8,128)(2,1)S(1)}, bf16[264,128]{1,0:T(8,128)(2,1)S(1)}, u32[]{:S(2)}, u32[]{:S(2)}) %collective-permute-start.9) | collective-permute-done | bytes 67616 | tf_op jit(solution)/shard_map/while/body/eval_jaxpr/ppermute | solution.py:30
  94.4 4.8 %collective-permute-start.1 = (bf16[264,128]{1,0:T(8,128)(2,1)S(1)}, bf16[264,128]{1,0:T(8,128)(2,1)S(1)}, u32[]{:S(2)}, u32[]{:S(2)}) collective-permute-start(bf16[264,128]{1,0:T(8,128)(2,1)S(1)} %get-tuple-element.1155.sent), channel_id=1, source_target_pairs={{16,36},{17,45},{24,44},{25,39},{18,38},{19,47},{26,46},{27,33},{2... | collective-permute-start | bytes 202760 | tf_op jit(solution)/shard_map/while/body/eval_jaxpr/ppermute | solution.py:30
  115.1 4.5 %collective-permute-done.9.refs_1_ = bf16[264,128]{1,0:T(8,128)(2,1)S(1)} collective-permute-done((bf16[264,128]{1,0:T(8,128)(2,1)S(1)}, bf16[264,128]{1,0:T(8,128)(2,1)S(1)}, u32[]{:S(2)}, u32[]{:S(2)}) %collective-permute-start.9) | collective-permute-done | bytes 67616 | tf_op jit(solution)/shard_map/while/body/eval_jaxpr/ppermute | solution.py:30
  197.8 67.1 %while.61 = (s32[]{:T(128)}, bf16[264,128]{1,0:T(8,128)(2,1)S(1)}, bf16[128,512]{1,0:T(8,128)(2,1)S(1)}, s32[7]{0:T(128)S(1)}, bf16[4,2,2,512,512]{4,3,2,1,0:T(8...) while((s32[]{:T(128)}, bf16[264,128]{1,0:T(8,128)(2,1)S(1)}, ...), condition=%wide.region_5.6_spmd, body=%wide.region_4.5_spmd.sunk | while | flops 9126805504 | bytes 37569160 | solution.py:345
  214.3 4.8 %collective-permute-done.20.refs_0_.refs_3_ = bf16[264,128]{1,0:T(8,128)(2,1)S(1)} collective-permute-done((bf16[264,128]{1,0:T(8,128)(2,1)S(1)}, bf16[264,128]{1,0:T(8,128)(2,1)S(1)}, u32[]{:S(2)}, u32[]{:S(2)}) %collective-permute-start.20) | collective-permute-done | bytes 67616 | tf_op jit(solution)/shard_map/while/body/eval_jaxpr/ppermute | solution.py:30
  219.1 4.3 collective-permute-done.21.refs_1_
  248.0 5.0 %collective-permute-done.20.refs_0_.refs_3_ = bf16[264,128]{1,0:T(8,128)(2,1)S(1)} collective-permute-done((bf16[264,128]{1,0:T(8,128)(2,1)S(1)}, bf16[264,128]{1,0:T(8,128)(2,1)S(1)}, u32[]{:S(2)}, u32[]{:S(2)}) %collective-permute-start.20) | collective-permute-done | bytes 67616 | tf_op jit(solution)/shard_map/while/body/eval_jaxpr/ppermute | solution.py:30
  253.0 5.0 %collective-permute-done.21.refs_1_ = bf16[264,128]{1,0:T(8,128)(2,1)S(1)} collective-permute-done((bf16[264,128]{1,0:T(8,128)(2,1)S(1)}, bf16[264,128]{1,0:T(8,128)(2,1)S(1)}, u32[]{:S(2)}, u32[]{:S(2)}) %collective-permute-start.21) | collective-permute-done | bytes 67616 | tf_op jit(solution)/shard_map/while/body/eval_jaxpr/ppermute | solution.py:30
  265.0 72.4 %while.62 = (s32[]{:T(128)}, bf16[264,128]{1,0:T(8,128)(2,1)S(1)}, bf16[128,512]{1,0:T(8,128)(2,1)S(1)}, s32[7]{0:T(128)S(1)}, bf16[4,2,2,512,512]{4,3,2,1,0:T(8...) while((s32[]{:T(128)}, bf16[264,128]{1,0:T(8,128)(2,1)S(1)}, ...), condition=%wide.region_7.8_spmd, body=%wide.region_6.7_spmd.sunk | while | flops 9126805504 | bytes 37569160 | solution.py:345
  281.6 5.0 %collective-permute-done.32.refs_0_.refs_3_ = bf16[264,128]{1,0:T(8,128)(2,1)S(1)} collective-permute-done((bf16[264,128]{1,0:T(8,128)(2,1)S(1)}, bf16[264,128]{1,0:T(8,128)(2,1)S(1)}, u32[]{:S(2)}, u32[]{:S(2)}) %collective-permute-start.32) | collective-permute-done | bytes 67616 | tf_op jit(solution)/shard_map/while/body/eval_jaxpr/ppermute | solution.py:30
  286.6 5.2 %collective-permute-done.33.refs_1_ = bf16[264,128]{1,0:T(8,128)(2,1)S(1)} collective-permute-done((bf16[264,128]{1,0:T(8,128)(2,1)S(1)}, bf16[264,128]{1,0:T(8,128)(2,1)S(1)}, u32[]{:S(2)}, u32[]{:S(2)}) %collective-permute-start.33) | collective-permute-done | bytes 67616 | tf_op jit(solution)/shard_map/while/body/eval_jaxpr/ppermute | solution.py:30
  314.9 11.2 %collective-permute-done.32.refs_0_.refs_3_ = bf16[264,128]{1,0:T(8,128)(2,1)S(1)} collective-permute-done((bf16[264,128]{1,0:T(8,128)(2,1)S(1)}, bf16[264,128]{1,0:T(8,128)(2,1)S(1)}, u32[]{:S(2)}, u32[]{:S(2)}) %collective-permute-start.32) | collective-permute-done | bytes 67616 | tf_op jit(solution)/shard_map/while/body/eval_jaxpr/ppermute | solution.py:30
  326.1 5.0 %collective-permute-done.33.refs_1_ = bf16[264,128]{1,0:T(8,128)(2,1)S(1)} collective-permute-done((bf16[264,128]{1,0:T(8,128)(2,1)S(1)}, bf16[264,128]{1,0:T(8,128)(2,1)S(1)}, u32[]{:S(2)}, u32[]{:S(2)}) %collective-permute-start.33) | collective-permute-done | bytes 67616 | tf_op jit(solution)/shard_map/while/body/eval_jaxpr/ppermute | solution.py:30
  337.4 107.9 %while.63 = (s32[]{:T(128)}, bf16[264,128]{1,0:T(8,128)(2,1)S(1)}, bf16[128,512]{1,0:T(8,128)(2,1)S(1)}, s32[7]{0:T(128)S(1)}, bf16[4,2,2,512,512]{4,3,2,1,0:T(8...) while((s32[]{:T(128)}, bf16[264,128]{1,0:T(8,128)(2,1)S(1)}, ...), condition=%wide.region_9.10_spmd, body=%wide.region_8.9_spmd.sunk | while | flops 9126805504 | bytes 37569160 | solution.py:345
  353.8 7.3 %collective-permute-done.44.refs_0_.refs_3_ = bf16[264,128]{1,0:T(8,128)(2,1)S(1)} collective-permute-done((bf16[264,128]{1,0:T(8,128)(2,1)S(1)}, bf16[264,128]{1,0:T(8,128)(2,1)S(1)}, u32[]{:S(2)}, u32[]{:S(2)}) %collective-permute-start.44) | collective-permute-done | bytes 67616 | tf_op jit(solution)/shard_map/while/body/eval_jaxpr/ppermute | solution.py:30
  389.9 7.0 %collective-permute-done.44.refs_0_.refs_3_ = bf16[264,128]{1,0:T(8,128)(2,1)S(1)} collective-permute-done((bf16[264,128]{1,0:T(8,128)(2,1)S(1)}, bf16[264,128]{1,0:T(8,128)(2,1)S(1)}, u32[]{:S(2)}, u32[]{:S(2)}) %collective-permute-start.44) | collective-permute-done | bytes 67616 | tf_op jit(solution)/shard_map/while/body/eval_jaxpr/ppermute | solution.py:30
  425.4 8.3 %collective-permute-done.44.refs_0_.refs_3_ = bf16[264,128]{1,0:T(8,128)(2,1)S(1)} collective-permute-done((bf16[264,128]{1,0:T(8,128)(2,1)S(1)}, bf16[264,128]{1,0:T(8,128)(2,1)S(1)}, u32[]{:S(2)}, u32[]{:S(2)}) %collective-permute-start.44) | collective-permute-done | bytes 67616 | tf_op jit(solution)/shard_map/while/body/eval_jaxpr/ppermute | solution.py:30
  433.7 4.5 %collective-permute-done.45.refs_1_ = bf16[264,128]{1,0:T(8,128)(2,1)S(1)} collective-permute-done((bf16[264,128]{1,0:T(8,128)(2,1)S(1)}, bf16[264,128]{1,0:T(8,128)(2,1)S(1)}, u32[]{:S(2)}, u32[]{:S(2)}) %collective-permute-start.45) | collective-permute-done | bytes 67616 | tf_op jit(solution)/shard_map/while/body/eval_jaxpr/ppermute | solution.py:30
  (415 shorter events, 325.0 us)
Async XLA Ops:
  12.0 41.3 %collective-permute-start.57 = (bf16[4,1024,512]{2,1,0:T(8,128)(2,1)}, bf16[4,1024,512]{2,1,0:T(8,128)(2,1)}, u32[]{:S(2)}, u32[]{:S(2)}) collective-permute-start(bf16[4,1024,512]{2,1,0:T(8,128)(2,1)} %stage.1), channel_id=1, source_target_pairs={{0,1},{1,0},{8,9},{9,8},{2,3},{3,2},{10,11},{11,10},{4,5},{5,4},{1... | collective-permute-start | bytes 12582920 | tf_op jit(solution)/shard_map/ppermute | solution.py:30
  19.9 28.4 %collective-permute-start.53 = (bf16[1024,128]{1,0:T(8,128)(2,1)S(1)}, bf16[1024,128]{1,0:T(8,128)(2,1)S(1)}, u32[]{:S(2)}, u32[]{:S(2)}) collective-permute-start(bf16[1024,128]{1,0:T(8,128)(2,1)S(1)} %get-tuple-element.803.after), channel_id=1, source_target_pairs={{0,4},{1,245},{8,12},{9,253},{2,6},{3,247},{10,14},{11,255},{4,0},... | collective-permute-start | bytes 786440 | tf_op jit(solution)/shard_map/ppermute | solution.py:30
  27.5 20.7 %collective-permute-start.52 = (bf16[1024,128]{1,0:T(8,128)(2,1)S(1)}, bf16[1024,128]{1,0:T(8,128)(2,1)S(1)}, u32[]{:S(2)}, u32[]{:S(2)}) collective-permute-start(bf16[1024,128]{1,0:T(8,128)(2,1)S(1)} %get-tuple-element.804), channel_id=1, source_target_pairs={{0,2},{1,243},{8,10},{9,251},{2,4},{3,245},{10,12},{11,253},{4,6},... | collective-permute-start | bytes 786440 | tf_op jit(solution)/shard_map/ppermute | solution.py:30
  30.0 20.7 %collective-permute-start.56 = (bf16[128,512]{1,0:T(8,128)(2,1)S(1)}, bf16[128,512]{1,0:T(8,128)(2,1)S(1)}, u32[]{:S(2)}, u32[]{:S(2)}) collective-permute-start(bf16[128,512]{1,0:T(8,128)(2,1)S(1)} %constant_dynamic-slice_fusion), channel_id=1, source_target_pairs={{0,1},{1,0},{8,9},{9,8},{2,3},{3,2},{10,11},{11,10},{4,5},{5,4},{1... | collective-permute-start | bytes 393224 | tf_op jit(solution)/shard_map/ppermute | solution.py:30
  207.7 19.2 %collective-permute-start.19 = (bf16[264,128]{1,0:T(8,128)(2,1)S(1)}, bf16[264,128]{1,0:T(8,128)(2,1)S(1)}, u32[]{:S(2)}, u32[]{:S(2)}) collective-permute-start(bf16[264,128]{1,0:T(8,128)(2,1)S(1)} %get-tuple-element.1097.sent), channel_id=1, source_target_pairs={{0,20},{1,29},{8,28},{9,23},{2,22},{3,31},{10,30},{11,17},{4,16},{... | collective-permute-start | bytes 202760 | tf_op jit(solution)/shard_map/while/body/eval_jaxpr/ppermute | solution.py:30
  209.0 19.0 %collective-permute-start.18 = (bf16[264,128]{1,0:T(8,128)(2,1)S(1)}, bf16[264,128]{1,0:T(8,128)(2,1)S(1)}, u32[]{:S(2)}, u32[]{:S(2)}) collective-permute-start(bf16[264,128]{1,0:T(8,128)(2,1)S(1)} %get-tuple-element.1097.sent), channel_id=1, source_target_pairs={{0,22},{1,31},{8,30},{9,17},{2,16},{3,25},{10,24},{11,19},{4,18},{... | collective-permute-start | bytes 202760 | tf_op jit(solution)/shard_map/while/body/eval_jaxpr/ppermute | solution.py:30
  241.4 18.8 %collective-permute-start.19 = (bf16[264,128]{1,0:T(8,128)(2,1)S(1)}, bf16[264,128]{1,0:T(8,128)(2,1)S(1)}, u32[]{:S(2)}, u32[]{:S(2)}) collective-permute-start(bf16[264,128]{1,0:T(8,128)(2,1)S(1)} %get-tuple-element.1097.sent), channel_id=1, source_target_pairs={{0,20},{1,29},{8,28},{9,23},{2,22},{3,31},{10,30},{11,17},{4,16},{... | collective-permute-start | bytes 202760 | tf_op jit(solution)/shard_map/while/body/eval_jaxpr/ppermute | solution.py:30
  242.7 18.6 %collective-permute-start.18 = (bf16[264,128]{1,0:T(8,128)(2,1)S(1)}, bf16[264,128]{1,0:T(8,128)(2,1)S(1)}, u32[]{:S(2)}, u32[]{:S(2)}) collective-permute-start(bf16[264,128]{1,0:T(8,128)(2,1)S(1)} %get-tuple-element.1097.sent), channel_id=1, source_target_pairs={{0,22},{1,31},{8,30},{9,17},{2,16},{3,25},{10,24},{11,19},{4,18},{... | collective-permute-start | bytes 202760 | tf_op jit(solution)/shard_map/while/body/eval_jaxpr/ppermute | solution.py:30
  273.7 18.1 %collective-permute-start.33 = (bf16[264,128]{1,0:T(8,128)(2,1)S(1)}, bf16[264,128]{1,0:T(8,128)(2,1)S(1)}, u32[]{:S(2)}, u32[]{:S(2)}) collective-permute-start(bf16[264,128]{1,0:T(8,128)(2,1)S(1)} %get-tuple-element.1116.sent), channel_id=1, source_target_pairs={{0,18},{1,27},{8,26},{9,21},{2,20},{3,29},{10,28},{11,23},{4,22},{... | collective-permute-start | bytes 202760 | tf_op jit(solution)/shard_map/while/body/eval_jaxpr/ppermute | solution.py:30
  275.0 18.8 %collective-permute-start.31 = (bf16[264,128]{1,0:T(8,128)(2,1)S(1)}, bf16[264,128]{1,0:T(8,128)(2,1)S(1)}, u32[]{:S(2)}, u32[]{:S(2)}) collective-permute-start(bf16[264,128]{1,0:T(8,128)(2,1)S(1)} %get-tuple-element.1116.sent), channel_id=1, source_target_pairs={{0,20},{1,29},{8,28},{9,23},{2,22},{3,31},{10,30},{11,17},{4,16},{... | collective-permute-start | bytes 202760 | tf_op jit(solution)/shard_map/while/body/eval_jaxpr/ppermute | solution.py:30
  276.3 18.5 %collective-permute-start.30 = (bf16[264,128]{1,0:T(8,128)(2,1)S(1)}, bf16[264,128]{1,0:T(8,128)(2,1)S(1)}, u32[]{:S(2)}, u32[]{:S(2)}) collective-permute-start(bf16[264,128]{1,0:T(8,128)(2,1)S(1)} %get-tuple-element.1116.sent), channel_id=1, source_target_pairs={{0,22},{1,31},{8,30},{9,17},{2,16},{3,25},{10,24},{11,19},{4,18},{... | collective-permute-start | bytes 202760 | tf_op jit(solution)/shard_map/while/body/eval_jaxpr/ppermute | solution.py:30
  305.7 20.4 %collective-permute-start.32 = (bf16[264,128]{1,0:T(8,128)(2,1)S(1)}, bf16[264,128]{1,0:T(8,128)(2,1)S(1)}, u32[]{:S(2)}, u32[]{:S(2)}) collective-permute-start(bf16[264,128]{1,0:T(8,128)(2,1)S(1)} %get-tuple-element.1116.sent), channel_id=1, source_target_pairs={{0,16},{1,25},{8,24},{9,19},{2,18},{3,27},{10,26},{11,21},{4,20},{... | collective-permute-start | bytes 202760 | tf_op jit(solution)/shard_map/while/body/eval_jaxpr/ppermute | solution.py:30
  307.0 24.1 %collective-permute-start.33 = (bf16[264,128]{1,0:T(8,128)(2,1)S(1)}, bf16[264,128]{1,0:T(8,128)(2,1)S(1)}, u32[]{:S(2)}, u32[]{:S(2)}) collective-permute-start(bf16[264,128]{1,0:T(8,128)(2,1)S(1)} %get-tuple-element.1116.sent), channel_id=1, source_target_pairs={{0,18},{1,27},{8,26},{9,21},{2,20},{3,29},{10,28},{11,23},{4,22},{... | collective-permute-start | bytes 202760 | tf_op jit(solution)/shard_map/while/body/eval_jaxpr/ppermute | solution.py:30
  308.3 24.4 %collective-permute-start.31 = (bf16[264,128]{1,0:T(8,128)(2,1)S(1)}, bf16[264,128]{1,0:T(8,128)(2,1)S(1)}, u32[]{:S(2)}, u32[]{:S(2)}) collective-permute-start(bf16[264,128]{1,0:T(8,128)(2,1)S(1)} %get-tuple-element.1116.sent), channel_id=1, source_target_pairs={{0,20},{1,29},{8,28},{9,23},{2,22},{3,31},{10,30},{11,17},{4,16},{... | collective-permute-start | bytes 202760 | tf_op jit(solution)/shard_map/while/body/eval_jaxpr/ppermute | solution.py:30
  309.6 24.1 %collective-permute-start.30 = (bf16[264,128]{1,0:T(8,128)(2,1)S(1)}, bf16[264,128]{1,0:T(8,128)(2,1)S(1)}, u32[]{:S(2)}, u32[]{:S(2)}) collective-permute-start(bf16[264,128]{1,0:T(8,128)(2,1)S(1)} %get-tuple-element.1116.sent), channel_id=1, source_target_pairs={{0,22},{1,31},{8,30},{9,17},{2,16},{3,25},{10,24},{11,19},{4,18},{... | collective-permute-start | bytes 202760 | tf_op jit(solution)/shard_map/while/body/eval_jaxpr/ppermute | solution.py:30
  345.9 19.4 %collective-permute-start.45 = (bf16[264,128]{1,0:T(8,128)(2,1)S(1)}, bf16[264,128]{1,0:T(8,128)(2,1)S(1)}, u32[]{:S(2)}, u32[]{:S(2)}) collective-permute-start(bf16[264,128]{1,0:T(8,128)(2,1)S(1)} %get-tuple-element.1135.sent), channel_id=1, source_target_pairs={{0,18},{1,27},{8,26},{9,21},{2,20},{3,29},{10,28},{11,23},{4,22},{... | collective-permute-start | bytes 202760 | tf_op jit(solution)/shard_map/while/body/eval_jaxpr/ppermute | solution.py:30
  347.2 21.5 %collective-permute-start.43 = (bf16[264,128]{1,0:T(8,128)(2,1)S(1)}, bf16[264,128]{1,0:T(8,128)(2,1)S(1)}, u32[]{:S(2)}, u32[]{:S(2)}) collective-permute-start(bf16[264,128]{1,0:T(8,128)(2,1)S(1)} %get-tuple-element.1135.sent), channel_id=1, source_target_pairs={{0,20},{1,29},{8,28},{9,23},{2,22},{3,31},{10,30},{11,17},{4,16},{... | collective-permute-start | bytes 202760 | tf_op jit(solution)/shard_map/while/body/eval_jaxpr/ppermute | solution.py:30
  348.5 21.2 %collective-permute-start.42 = (bf16[264,128]{1,0:T(8,128)(2,1)S(1)}, bf16[264,128]{1,0:T(8,128)(2,1)S(1)}, u32[]{:S(2)}, u32[]{:S(2)}) collective-permute-start(bf16[264,128]{1,0:T(8,128)(2,1)S(1)} %get-tuple-element.1135.sent), channel_id=1, source_target_pairs={{0,22},{1,31},{8,30},{9,17},{2,16},{3,25},{10,24},{11,19},{4,18},{... | collective-permute-start | bytes 202760 | tf_op jit(solution)/shard_map/while/body/eval_jaxpr/ppermute | solution.py:30
  382.0 18.0 %collective-permute-start.45 = (bf16[264,128]{1,0:T(8,128)(2,1)S(1)}, bf16[264,128]{1,0:T(8,128)(2,1)S(1)}, u32[]{:S(2)}, u32[]{:S(2)}) collective-permute-start(bf16[264,128]{1,0:T(8,128)(2,1)S(1)} %get-tuple-element.1135.sent), channel_id=1, source_target_pairs={{0,18},{1,27},{8,26},{9,21},{2,20},{3,29},{10,28},{11,23},{4,22},{... | collective-permute-start | bytes 202760 | tf_op jit(solution)/shard_map/while/body/eval_jaxpr/ppermute | solution.py:30
  383.3 20.9 %collective-permute-start.43 = (bf16[264,128]{1,0:T(8,128)(2,1)S(1)}, bf16[264,128]{1,0:T(8,128)(2,1)S(1)}, u32[]{:S(2)}, u32[]{:S(2)}) collective-permute-start(bf16[264,128]{1,0:T(8,128)(2,1)S(1)} %get-tuple-element.1135.sent), channel_id=1, source_target_pairs={{0,20},{1,29},{8,28},{9,23},{2,22},{3,31},{10,30},{11,17},{4,16},{... | collective-permute-start | bytes 202760 | tf_op jit(solution)/shard_map/while/body/eval_jaxpr/ppermute | solution.py:30
  384.6 20.7 %collective-permute-start.42 = (bf16[264,128]{1,0:T(8,128)(2,1)S(1)}, bf16[264,128]{1,0:T(8,128)(2,1)S(1)}, u32[]{:S(2)}, u32[]{:S(2)}) collective-permute-start(bf16[264,128]{1,0:T(8,128)(2,1)S(1)} %get-tuple-element.1135.sent), channel_id=1, source_target_pairs={{0,22},{1,31},{8,30},{9,17},{2,16},{3,25},{10,24},{11,19},{4,18},{... | collective-permute-start | bytes 202760 | tf_op jit(solution)/shard_map/while/body/eval_jaxpr/ppermute | solution.py:30
  417.5 20.7 %collective-permute-start.45 = (bf16[264,128]{1,0:T(8,128)(2,1)S(1)}, bf16[264,128]{1,0:T(8,128)(2,1)S(1)}, u32[]{:S(2)}, u32[]{:S(2)}) collective-permute-start(bf16[264,128]{1,0:T(8,128)(2,1)S(1)} %get-tuple-element.1135.sent), channel_id=1, source_target_pairs={{0,18},{1,27},{8,26},{9,21},{2,20},{3,29},{10,28},{11,23},{4,22},{... | collective-permute-start | bytes 202760 | tf_op jit(solution)/shard_map/while/body/eval_jaxpr/ppermute | solution.py:30
  418.8 21.8 %collective-permute-start.43 = (bf16[264,128]{1,0:T(8,128)(2,1)S(1)}, bf16[264,128]{1,0:T(8,128)(2,1)S(1)}, u32[]{:S(2)}, u32[]{:S(2)}) collective-permute-start(bf16[264,128]{1,0:T(8,128)(2,1)S(1)} %get-tuple-element.1135.sent), channel_id=1, source_target_pairs={{0,20},{1,29},{8,28},{9,23},{2,22},{3,31},{10,30},{11,17},{4,16},{... | collective-permute-start | bytes 202760 | tf_op jit(solution)/shard_map/while/body/eval_jaxpr/ppermute | solution.py:30
  420.1 21.5 %collective-permute-start.42 = (bf16[264,128]{1,0:T(8,128)(2,1)S(1)}, bf16[264,128]{1,0:T(8,128)(2,1)S(1)}, u32[]{:S(2)}, u32[]{:S(2)}) collective-permute-start(bf16[264,128]{1,0:T(8,128)(2,1)S(1)} %get-tuple-element.1135.sent), channel_id=1, source_target_pairs={{0,22},{1,31},{8,30},{9,17},{2,16},{3,25},{10,24},{11,19},{4,18},{... | collective-permute-start | bytes 202760 | tf_op jit(solution)/shard_map/while/body/eval_jaxpr/ppermute | solution.py:30
  (126 other events, 669.0 us)
